TPU v7x, 32 devices: a whole 2x2x4 slice. The times are simulated.
32 devices in a mesh: dap: 8 (over z, x), cplx: 4 (over y, core).
Axes of the slice: x: 2, y: 2, z: 4, core: 2. Of those that a mesh axis runs over, the one named last changes fastest.
Arguments:
- pair: bfloat16 [96, 384, 128], P('dap', 'cplx'), parts along dimension 1, may hold values from -6 to 6
- cotangent: bfloat16 [96, 384, 128], P('dap', 'cplx'), parts along dimension 1, may hold values from -6 to 6
- residue_mask: int32 [384], P('cplx'), parts along dimension 0, may hold values 0 or 1
- chain_ids: int32 [384], P('cplx'), parts along dimension 0, may hold values from 0 to 2, never falling along the last dimension, each value on 1 to 48 neighbouring positions
- chain_embed: float32 [2, 128], replicated, may hold values from -4 to 4
- out_norm_gain: float32 [128], replicated, may hold values from 0.25 to 1.75
- out_proj: bfloat16 [128, 512], replicated, may hold values from -0.5 to 0.5
- out_gate: bfloat16 [128, 128], replicated, may hold values from -0.5 to 0.5
- out_mid_gain: float32 [128], replicated, may hold values from 0.25 to 1.75
- out_final: bfloat16 [128, 128], replicated, may hold values from -0.5 to 0.5
- in_norm_gain: float32 [128], replicated, may hold values from 0.25 to 1.75
- in_proj: bfloat16 [128, 512], replicated, may hold values from -0.5 to 0.5
- in_gate: bfloat16 [128, 128], replicated, may hold values from -0.5 to 0.5
- in_mid_gain: float32 [128], replicated, may hold values from 0.25 to 1.75
- in_final: bfloat16 [128, 128], replicated, may hold values from -0.5 to 0.5
Outputs:
- pair_grad: bfloat16 [96, 384, 128], P('dap', 'cplx'), parts along dimension 1
- grad_proj: float32 [512, 512], P('cplx'), parts along dimension 0
- grad_gate: float32 [512, 128], P('cplx'), parts along dimension 0
- grad_final: float32 [512, 128], P('cplx'), parts along dimension 0
- grad_norm_gain: float32 [512], P('cplx'), parts along dimension 0
- grad_mid_gain: float32 [512], P('cplx'), parts along dimension 0
There are 4 independent parts, one for each index of `cplx`. A program takes and returns all parts, laid end to end along the dimension named above; an argument that names none is the same for every part. Nothing has to cross between parts.
Inputs may be any that keep to these rules, and one draw needn't show every extreme that they name: `chain_ids`: chain numbers never fall along the residues; each chain has at most 48 residues.
All inputs are finite; a program needn't handle non-finite values.
Results may differ from a plain program's by a relative error of at most 0.019.
Values may be sent and summed in bfloat16 or wider, within the bound.
A program may use at most 128 MiB of HBM per device.

v0:
```python
import jax
import jax.numpy as jnp
from jax import lax
from jax.sharding import PartitionSpec as P


def layer_norm(values_in, gain):
    average = jnp.mean(values_in, axis=-1, keepdims=True)
    centred = values_in - average
    variance = jnp.mean(centred * centred, axis=-1, keepdims=True)
    return centred * lax.rsqrt(variance + 1e-05) * gain


def gated_pair(projected, pair_mask, hidden_width):
    masked = pair_mask[..., None]
    left_act = (
        masked
        * jax.nn.sigmoid(projected[..., :hidden_width])
        * projected[..., hidden_width : 2 * hidden_width]
    )
    right_act = (
        masked
        * jax.nn.sigmoid(projected[..., 2 * hidden_width : 3 * hidden_width])
        * projected[..., 3 * hidden_width :]
    )
    return (left_act, right_act)


def shards(
    pair,
    cotangent,
    residue_mask,
    chain_ids,
    chain_embed,
    out_norm_gain,
    out_proj,
    out_gate,
    out_mid_gain,
    out_final,
    in_norm_gain,
    in_proj,
    in_gate,
    in_mid_gain,
    in_final,
):
    f32 = jnp.float32
    bf16 = jnp.bfloat16
    row_count = pair.shape[0]
    res_count = pair.shape[1]
    hidden_width = out_final.shape[0]
    inv_count = 1.0 / res_count
    row_start = lax.axis_index("dap") * row_count
    row_mask = lax.dynamic_slice_in_dim(residue_mask, row_start, row_count, 0)
    row_chain = lax.dynamic_slice_in_dim(chain_ids, row_start, row_count, 0)
    pair_mask = (row_mask[:, None] * residue_mask[None, :]).astype(f32)
    same_chain = row_chain[:, None] == chain_ids[None, :]
    start = pair.astype(f32) + jnp.where(same_chain[..., None], chain_embed[1], chain_embed[0])
    out_normed = layer_norm(start, out_norm_gain).astype(bf16)
    projected = jnp.dot(out_normed, out_proj, preferred_element_type=f32)
    left_act, right_act = gated_pair(projected, pair_mask, hidden_width)
    left_b = left_act.astype(bf16)
    right_b = right_act.astype(bf16)
    x_out = jnp.einsum(
        "ikc,jkc->ijc",
        left_b,
        lax.all_gather(right_b, "dap", axis=0, tiled=True),
        preferred_element_type=f32,
    )
    y_out = layer_norm(x_out, out_mid_gain).astype(bf16)
    update = jax.nn.sigmoid(jnp.dot(out_normed, out_gate, preferred_element_type=f32)) * jnp.dot(
        y_out, out_final, preferred_element_type=f32
    )
    pair_mid = (start + update).astype(bf16)
    mid_f32 = pair_mid.astype(f32)
    normed_f32, norm_back = jax.vjp(layer_norm, mid_f32, in_norm_gain)
    in_normed = normed_f32.astype(bf16)
    proj_in = jnp.dot(in_normed, in_proj, preferred_element_type=f32)
    (left_in, right_in), glu_back = jax.vjp(
        lambda proj_val: gated_pair(proj_val, pair_mask, hidden_width), proj_in
    )
    left_ib = left_in.astype(bf16)
    right_ib = right_in.astype(bf16)
    columns = lax.all_to_all(left_ib, "dap", split_axis=1, concat_axis=0, tiled=True)
    left_block = columns
    x_in = jnp.einsum(
        "kic,kjc->ijc",
        left_block,
        lax.all_gather(right_ib, "dap", axis=0, tiled=True),
        preferred_element_type=f32,
    )
    y_f32, mid_back = jax.vjp(layer_norm, x_in, in_mid_gain)
    y_in = y_f32.astype(bf16)
    logit = jnp.dot(in_normed, in_gate, preferred_element_type=f32)
    value = jnp.dot(y_in, in_final, preferred_element_type=f32)
    sigma = jax.nn.sigmoid(logit)
    upstream = cotangent.astype(f32)
    grad_value = (upstream * sigma).astype(bf16)
    grad_logit = (upstream * value * sigma * (1.0 - sigma)).astype(bf16)
    grad_final = jnp.einsum("ijc,ijd->cd", y_in, grad_value, preferred_element_type=f32) * inv_count
    grad_gate = (
        jnp.einsum("ijc,ijd->cd", in_normed, grad_logit, preferred_element_type=f32) * inv_count
    )
    grad_y = jnp.dot(grad_value, in_final.T, preferred_element_type=f32)
    grad_x, grad_mid = mid_back(grad_y)
    grad_x_b = grad_x.astype(bf16)
    shard_rows = lax.all_gather(grad_x_b, "dap", axis=0, tiled=True)
    left_block = left_ib
    grad_right = jnp.einsum("kic,ijc->kjc", left_block, shard_rows, preferred_element_type=f32)
    new_block = jnp.einsum("kjc,ijc->kic", right_ib, shard_rows, preferred_element_type=f32)
    grad_p = glu_back((new_block, grad_right))[0].astype(bf16)
    grad_proj = jnp.einsum("ijc,ijd->cd", in_normed, grad_p, preferred_element_type=f32) * inv_count
    grad_normed = jnp.dot(grad_p, in_proj.T, preferred_element_type=f32) + jnp.dot(
        grad_logit, in_gate.T, preferred_element_type=f32
    )
    grad_z, grad_norm = norm_back(grad_normed)
    pair_grad = (upstream + grad_z).astype(bf16)
    reduced = (
        lax.psum(grad_proj.astype(jnp.bfloat16), "dap").astype(jnp.float32),
        lax.psum(grad_gate.astype(jnp.bfloat16), "dap").astype(jnp.float32),
        lax.psum(grad_final.astype(jnp.bfloat16), "dap").astype(jnp.float32),
        lax.psum((grad_norm * inv_count).astype(jnp.bfloat16), "dap").astype(jnp.float32),
        lax.psum((grad_mid * inv_count).astype(jnp.bfloat16), "dap").astype(jnp.float32),
    )
    return (pair_grad, reduced[0], reduced[1], reduced[2], reduced[3], reduced[4])


def solution(mesh):
    placed = (
        P("dap", "cplx", None),
        P("dap", "cplx", None),
        P("cplx"),
        P("cplx"),
        P(),
        P(),
        P(),
        P(),
        P(),
        P(),
        P(),
        P(),
        P(),
        P(),
        P(),
    )
    return jax.shard_map(
        shards,
        mesh=mesh,
        in_specs=placed,
        out_specs=(
            P("dap", "cplx", None),
            P("cplx", None),
            P("cplx", None),
            P("cplx", None),
            P("cplx"),
            P("cplx"),
        ),
        check_vma=False,
    )
```

profile of v0, /device:TPU:0, one launch (start us, length us, event | category | flops | bytes accessed | tf_op | source)
XLA Modules:
  0.0 371.3 jit_solution(1143531026395006253)
XLA Ops:
  9.5 1.4 fusion.41
  10.9 1.6 multiply_reduce_fusion.7
  13.9 1.9 fusion.47
  17.0 1.2 copy.47
  18.3 1.7 fusion.8
  19.9 51.8 %all-gather.4.cloned.1.call-done = bf16[96,96,128]{2,1,0:T(8,128)(2,1)} async-done(((bf16[12,96,128]{2,1,0:T(8,128)(2,1)}), bf16[96,96,128]{2,1,0:T(8,128)(2,1)}) %all-gather.4.cloned.1.call-update) | async-done | bytes 2359312 | tf_op jit(solution)/shard_map/all_gather | solution.py:66
  71.7 3.5 copy.46
  75.2 2.8 fusion.62
  81.5 1.4 copy-done.1
  84.9 3.5 all-to-all-start
  89.5 17.3 %all-to-all-done = bf16[12,96,128]{2,0,1:T(8,128)(2,1)S(1)} async-done(((bf16[12,96,128]{2,0,1:T(8,128)(2,1)}), bf16[12,96,128]{2,0,1:T(8,128)(2,1)S(1)}, u32[]{:S(2)}, u32[]{:S(2)}) %all-to-all-start) | async-done | bytes 294944 | tf_op jit(solution)/shard_map/all_to_all | solution.py:83
  107.0 1.2 copy.53
  108.2 29.5 %all-gather.6.cloned.1.call-done = bf16[96,96,128]{2,1,0:T(8,128)(2,1)} async-done(((bf16[12,96,128]{2,1,0:T(8,128)(2,1)}), bf16[96,96,128]{2,1,0:T(8,128)(2,1)}) %all-gather.6.cloned.1.call-update) | async-done | bytes 2359312 | tf_op jit(solution)/shard_map/all_gather | solution.py:88
  137.7 3.5 copy.52
  141.3 3.0 fusion.64
  144.2 1.6 copy.54
  147.7 1.5 add_convert_fusion.1
  150.6 1.2 copy.56
  154.4 1.3 fusion.17
  155.7 44.1 %all-gather.8.cloned.1.call-done = bf16[96,96,128]{2,1,0:T(8,128)(2,1)} async-done(((bf16[12,96,128]{2,1,0:T(8,128)(2,1)}), bf16[96,96,128]{2,1,0:T(8,128)(2,1)}) %all-gather.8.cloned.1.call-update) | async-done | bytes 2359312 | tf_op jit(solution)/shard_map/all_gather | solution.py:106
  199.8 3.5 copy.55
  203.3 3.8 %fusion.66 = f32[128,96,12]{1,2,0:T(8,128)} fusion(bf16[96,96,128]{1,0,2:T(8,128)(2,1)S(1)} %copy.55, bf16[12,96,128]{1,0,2:T(8,128)(2,1)} %copy.59), kind=kOutput, calls=%fused_computation.126 | convolution fusion | flops 28311552 | bytes 3244032 | tf_op jit(solution)/shard_map/kjc,ijc->kic/dot_general | solution.py:109
  207.1 2.4 copy.60
  209.4 2.9 fusion.65
  212.4 1.5 copy.57
  213.9 2.4 bitcast_multiply_fusion.3
  220.8 1.5 fusion.19
  222.3 66.6 %all-reduce.10.cloned.1.call-done = (bf16[128,128]{1,0:T(8,128)(2,1)}, bf16[128,128]{1,0:T(8,128)(2,1)}, bf16[128]{0:T(256)(128)(2,1)}, bf16[128]{0:T(256)(128)(2,1)}) async-done(((bf16[128,128]{1,0:T(8,128)(2,1)}, bf16[128,128]{1,0:T(8,128)(2,1)}, bf16[128]{0:T(256)(128)(2,1)}, bf16[128]{0:T(256)(128)(2,1)}), (bf16[128,128]{1,0:T(8,128)(2,1)}, bf16[128,128]{1,0:T(8,128)(2,1)}, bf16[128]{0:T(256)(128)(2,1)}, ...) | async-done | bytes 66064 | tf_op jit(solution)/shard_map/psum | solution.py:119
  288.9 1.4 convert_element_type.109
  290.3 1.4 convert_element_type.111
  293.9 69.3 %all-reduce.8.cloned.1.call-done = bf16[128,512]{1,0:T(8,128)(2,1)} async-done(((bf16[128,512]{1,0:T(8,128)(2,1)}), bf16[128,512]{1,0:T(8,128)(2,1)}) %all-reduce.8.cloned.1.call-update) | async-done | bytes 131088 | tf_op jit(solution)/shard_map/psum | solution.py:118
  363.2 1.6 convert_element_type.107
  (103 shorter events, 24.0 us)
Async XLA Ops:
  7.2 73.9 %copy-start = (bf16[128,512]{1,0:T(8,128)(2,1)S(1)}, bf16[128,512]{1,0:T(8,128)(2,1)}, u32[]{:S(2)}) copy-start(bf16[128,512]{1,0:T(8,128)(2,1)} %param.26) | copy-start | bytes 393220
  7.2 64.5 %all-gather.4.cloned.1.call-start = ((), (), s32[]{:S(2)}) async-start(), calls=%async_computation.1 | async-start | bytes 2654208 | tf_op jit(solution)/shard_map/all_gather | solution.py:66
  15.9 2.4 copy-start.5
  15.9 2.4 copy-start.23
  15.9 2.4 copy-start.25
  17.0 120.7 %all-gather.6.cloned.1.call-start = ((), (), s32[]{:S(2)}) async-start(), calls=%async_computation.2 | async-start | bytes 2654208 | tf_op jit(solution)/shard_map/all_gather | solution.py:88
  75.2 3.1 copy-start.24
  78.0 1.0 copy-start.6
  78.0 1.2 copy-start.17
  78.0 1.2 copy-start.19
  78.1 2.6 copy-start.22
  79.8 0.8 copy-start.2
  81.1 7.4 %copy-start.14 = (bf16[12,96,128]{2,1,0:T(8,128)(2,1)}, bf16[12,96,128]{2,1,0:T(8,128)(2,1)S(1)}, u32[]{:S(2)}) copy-start(bf16[12,96,128]{2,1,0:T(8,128)(2,1)S(1)} %multiply_convert_fusion.4) | copy-start | bytes 884740
  81.5 1.4 copy-start.1
  82.9 5.5 %copy-start.20 = (bf16[128,128]{1,0:T(8,128)(2,1)S(1)}, bf16[128,128]{1,0:T(8,128)(2,1)}, u32[]{:S(2)}) copy-start(bf16[128,128]{1,0:T(8,128)(2,1)} %param.27) | copy-start | bytes 98308
  84.0 22.9 %copy-start.9 = (bf16[12,96,128]{2,1,0:T(8,128)(2,1)}, bf16[12,96,128]{2,1,0:T(8,128)(2,1)S(1)}, u32[]{:S(2)}) copy-start(bf16[12,96,128]{2,1,0:T(8,128)(2,1)S(1)} %get-tuple-element.22) | copy-start | bytes 884740
  84.9 22.0 %all-to-all-start = ((bf16[12,96,128]{2,0,1:T(8,128)(2,1)}), bf16[12,96,128]{2,0,1:T(8,128)(2,1)S(1)}, u32[]{:S(2)}, u32[]{:S(2)}) async-start(bf16[12,96,128]{2,0,1:T(8,128)(2,1)} %copy.49), calls=%async_computation | async-start | bytes 786432 | tf_op jit(solution)/shard_map/all_to_all | solution.py:83
  88.4 111.4 %all-gather.8.cloned.1.call-start = ((), (), s32[]{:S(2)}) async-start(), calls=%async_computation.3 | async-start | bytes 2654208 | tf_op jit(solution)/shard_map/all_gather | solution.py:106
  141.2 4.9 %copy-start.18 = (bf16[128,128]{1,0:T(8,128)(2,1)S(1)}, bf16[128,128]{1,0:T(8,128)(2,1)}, u32[]{:S(2)}) copy-start(bf16[128,128]{1,0:T(8,128)(2,1)} %param.29) | copy-start | bytes 98308
  141.2 4.9 %copy-start.21 = (f32[128]{0:T(128)S(1)}, f32[128]{0:T(128)}, u32[]{:S(2)}) copy-start(f32[128]{0:T(128)} %param.28) | copy-start | bytes 1540
  144.2 1.9 copy-start.4
  144.2 1.9 copy-start.7
  146.2 3.2 copy-start.11
  146.9 3.7 %copy-start.10 = (bf16[12,96,128]{2,1,0:T(8,128)(2,1)S(1)}, bf16[12,96,128]{2,1,0:T(8,128)(2,1)}, u32[]{:S(2)}) copy-start(bf16[12,96,128]{2,1,0:T(8,128)(2,1)} %copy-done.9) | copy-start | bytes 884740
  147.7 5.9 %copy-start.15 = (bf16[12,96,128]{2,1,0:T(8,128)(2,1)S(1)}, bf16[12,96,128]{2,1,0:T(8,128)(2,1)}, u32[]{:S(2)}) copy-start(bf16[12,96,128]{2,1,0:T(8,128)(2,1)} %copy-done.14) | copy-start | bytes 884740
  149.2 139.7 %all-reduce.10.cloned.1.call-start = ((), (), s32[]{:S(2)}) async-start(), calls=%async_computation.5 | async-start | bytes 133120 | tf_op jit(solution)/shard_map/psum | solution.py:119
  152.8 0.7 copy-start.12
  216.3 1.0 copy-start.16
  217.3 1.1 copy-start.3
  217.3 1.1 copy-start.13
  218.3 2.5 copy-start.8
  220.2 143.0 %all-reduce.8.cloned.1.call-start = ((), (), s32[]{:S(2)}) async-start(), calls=%async_computation.4 | async-start | bytes 262144 | tf_op jit(solution)/shard_map/psum | solution.py:118
Sparse Core Ops, SparseCore 0:
  17.1 54.5 all-gather.3
  84.1 53.5 all-gather.5
  149.3 50.4 all-gather.7
  220.3 68.4 all-reduce.9
  292.6 70.4 all-reduce.7
where the time goes:
time: 372 us; the launch traced here: 371 us
  waiting for transfers between devices  279 us (75%)
  local copies, waits for them, and re-layouts  27.9 us (8%)
  matrix products  23.6 us (6%)
  other arithmetic  22.7 us (6%)
  between operations  14.2 us (4%)
  starting transfers between devices  3.84 us (1%)
    psum x1, waiting for transfers between devices, shards(): lax.psum(grad_proj.astype(jnp.bfloat16), 'dap').astype(jnp.float32)  69.3 us
    psum x1, waiting for transfers between devices, shards(): lax.psum(grad_gate.astype(jnp.bfloat16), 'dap').astype(jnp.float32)  66.6 us
    all_gather x1, waiting for transfers between devices, shards(): lax.all_gather(right_b, 'dap', axis=0, tiled=True)  51.8 us
    all_gather x1, waiting for transfers between devices, shards(): shard_rows = lax.all_gather(grad_x_b, 'dap', axis=0, tiled=True)  44.1 us
    all_gather x1, waiting for transfers between devices, shards(): lax.all_gather(right_ib, 'dap', axis=0, tiled=True)  29.5 us
    all_to_all x1, waiting for transfers between devices, shards(): lax.all_to_all(left_ib, 'dap', split_axis=1, concat_axis=0, tiled=True)  17.3 us
  transfers between devices with their start and end apart: 6, of which 6 were waited for; matrix products, arithmetic and copies ran while one was open for 5% of the time, Pallas kernels for 0%

commit v1 on v0

--- a/solution.py
+++ b/solution.py
@@ -82,12 +82,38 @@
     right_ib = right_in.astype(bf16)
     columns = lax.all_to_all(left_ib, "dap", split_axis=1, concat_axis=0, tiled=True)
     left_block = columns
-    x_in = jnp.einsum(
+    size, index, rows = (lax.axis_size("dap"), lax.axis_index("dap"), right_ib.shape[0])
+    right = [(i, (i + 1) % size) for i in range(size)]
+    left = [(i, (i - 1) % size) for i in range(size)]
+    halfway = size // 2
+    from_left = from_right = right_ib
+    subtotal = jnp.einsum(
         "kic,kjc->ijc",
-        left_block,
-        lax.all_gather(right_ib, "dap", axis=0, tiled=True),
+        lax.dynamic_slice_in_dim(left_block, index * rows, right_ib.shape[0], axis=0),
+        right_ib,
         preferred_element_type=f32,
     )
+    for step in range(1, halfway + 1):
+        from_left = lax.ppermute(from_left, "dap", right)
+        if step < size - halfway:
+            from_right = lax.ppermute(from_right, "dap", left)
+            subtotal = subtotal + jnp.einsum(
+                "kic,kjc->ijc",
+                lax.dynamic_slice_in_dim(
+                    left_block, (index + step) % size * rows, from_right.shape[0], axis=0
+                ),
+                from_right,
+                preferred_element_type=f32,
+            )
+        subtotal = subtotal + jnp.einsum(
+            "kic,kjc->ijc",
+            lax.dynamic_slice_in_dim(
+                left_block, (index - step) % size * rows, from_left.shape[0], axis=0
+            ),
+            from_left,
+            preferred_element_type=f32,
+        )
+    x_in = subtotal
     y_f32, mid_back = jax.vjp(layer_norm, x_in, in_mid_gain)
     y_in = y_f32.astype(bf16)
     logit = jnp.dot(in_normed, in_gate, preferred_element_type=f32)

time: 372 us -> 390 us (1.048)
  local copies, waits for them, and re-layouts: 27.9 us -> 53.6 us
  waiting for transfers between devices: 279 us -> 254 us
  starting transfers between devices: 3.84 us -> 14.7 us
  matrix products: 23.6 us -> 27.8 us
    all_gather x1 -> x0, waiting for transfers between devices: 29.5 us -> none  [shards(): lax.all_gather(right_ib, 'dap', axis=0, tiled=True)]
    ppermute x0 -> x7, waiting for transfers between devices: none -> 18.6 us  [the longest x3 14.2 us: shards(): from_right = lax.ppermute(from_right, 'dap', left)]
    all_to_all x1, waiting for transfers between devices: 17.3 us -> 0.01 us  [shards(): lax.all_to_all(left_ib, 'dap', split_axis=1, concat_axis=0, tiled=True)]
    ppermute x0 -> x7, local copies, waits for them, and re-layouts: none -> 13.6 us  [the longest x4 7.89 us: shards(): from_left = lax.ppermute(from_left, 'dap', right)]
    ppermute x0 -> x7, starting transfers between devices: none -> 11.1 us  [the longest x3 9.21 us: shards(): from_right = lax.ppermute(from_right, 'dap', left)]
    unnamed x52 -> x86, local copies, waits for them, and re-layouts: 3.78 us -> 13.5 us
    dot_general x1 -> x8, local copies, waits for them, and re-layouts: 1.62 us -> 8.69 us  [the longest x4 4.75 us: shards(): jnp.einsum('kic,kjc->ijc', lax.dynamic_slice_in_dim(left_block, (index -...]
    dot_general x1 -> x8, matrix products: 2.96 us -> 7.93 us  [the longest x4 4.57 us: shards(): jnp.einsum('kic,kjc->ijc', lax.dynamic_slice_in_dim(left_block, (index -...]
  transfers between devices with their start and end apart: 6 -> 12, of which waited for: 6 -> 7; matrix products, arithmetic and copies ran while one was open for 5% -> 13% of each run, Pallas kernels for 0% -> 0%
where the time goes in v1:
time: 390 us; the launch traced here: 388 us
  waiting for transfers between devices  254 us (65%)
  local copies, waits for them, and re-layouts  53.6 us (14%)
  matrix products  27.8 us (7%)
  other arithmetic  23.8 us (6%)
  starting transfers between devices  14.7 us (4%)
  between operations  14.4 us (4%)
    psum x1, waiting for transfers between devices, shards(): lax.psum(grad_proj.astype(jnp.bfloat16), 'dap').astype(jnp.float32)  69.2 us
    psum x1, waiting for transfers between devices, shards(): lax.psum(grad_gate.astype(jnp.bfloat16), 'dap').astype(jnp.float32)  66.6 us
    all_gather x1, waiting for transfers between devices, shards(): lax.all_gather(right_b, 'dap', axis=0, tiled=True)  51.9 us
    all_gather x1, waiting for transfers between devices, shards(): shard_rows = lax.all_gather(grad_x_b, 'dap', axis=0, tiled=True)  46.9 us
    ppermute x3, waiting for transfers between devices, shards(): from_right = lax.ppermute(from_right, 'dap', left)  14.2 us
    unnamed x86, local copies, waits for them, and re-layouts  13.5 us
    ppermute x3, starting transfers between devices, shards(): from_right = lax.ppermute(from_right, 'dap', left)  9.21 us
    ppermute x4, local copies, waits for them, and re-layouts, shards(): from_left = lax.ppermute(from_left, 'dap', right)  7.89 us
  transfers between devices with their start and end apart: 12, of which 7 were waited for; matrix products, arithmetic and copies ran while one was open for 13% of the time, Pallas kernels for 0%

profile of v1, /device:TPU:0, one launch (start us, length us, event | category | flops | bytes accessed | tf_op | source)
XLA Modules:
  0.0 388.1 jit_solution(10983464398136637770)
XLA Ops:
  10.9 1.6 multiply_reduce_fusion.7
  13.9 1.9 fusion.47
  18.2 1.6 fusion.8
  19.8 51.9 %all-gather.3.cloned.1.call-done = bf16[96,96,128]{2,1,0:T(8,128)(2,1)} async-done(((bf16[12,96,128]{2,1,0:T(8,128)(2,1)}), bf16[96,96,128]{2,1,0:T(8,128)(2,1)}) %all-gather.3.cloned.1.call-update) | async-done | bytes 2359312 | tf_op jit(solution)/shard_map/all_gather | solution.py:66
  71.7 3.5 copy.81
  75.2 2.8 fusion.62
  84.9 3.5 all-to-all-start
  88.4 4.6 %collective-permute-start = (bf16[12,96,128]{2,1,0:T(8,128)(2,1)S(1)}, bf16[12,96,128]{2,1,0:T(8,128)(2,1)}, u32[]{:S(2)}, u32[]{:S(2)}) collective-permute-start(bf16[12,96,128]{2,1,0:T(8,128)(2,1)S(1)} %get-tuple-element.25), channel_id=1, source_target_pairs={{0,28},{4,0},{8,4},{12,8},{16,12},{20,16},{24,20},{28,24},{1,29},{... | collective-permute-start | bytes 884744 | tf_op jit(solution)/shard_map/ppermute | solution.py:99
  93.8 14.2 %collective-permute-done = bf16[12,96,128]{2,1,0:T(8,128)(2,1)} collective-permute-done((bf16[12,96,128]{2,1,0:T(8,128)(2,1)S(1)}, bf16[12,96,128]{2,1,0:T(8,128)(2,1)}, u32[]{:S(2)}, u32[]{:S(2)}) %collective-permute-start) | collective-permute-done | bytes 294944 | tf_op jit(solution)/shard_map/ppermute | solution.py:99
  110.3 2.2 copy.94
  122.1 2.1 copy.122
  124.1 2.0 copy.123
  128.3 2.2 copy.97
  130.5 3.6 collective-permute-start.4
  134.1 1.5 fusion.67
  136.8 2.2 copy.100
  139.0 1.5 fusion.68
  141.6 2.2 copy.103
  150.4 4.0 %collective-permute-done.6 = bf16[12,96,128]{2,1,0:T(8,128)(2,1)} collective-permute-done((bf16[12,96,128]{2,1,0:T(8,128)(2,1)}, bf16[12,96,128]{2,1,0:T(8,128)(2,1)}, u32[]{:S(2)}, u32[]{:S(2)}) %collective-permute-start.6) | collective-permute-done | bytes 294944 | tf_op jit(solution)/shard_map/ppermute | solution.py:97
  154.4 2.2 copy.109
  156.5 1.5 fusion.71
  159.3 2.1 bitcast_reduce_fusion
  169.6 46.9 %all-gather.5.cloned.1.call-done = bf16[96,96,128]{2,1,0:T(8,128)(2,1)} async-done(((bf16[12,96,128]{2,1,0:T(8,128)(2,1)}), bf16[96,96,128]{2,1,0:T(8,128)(2,1)}) %all-gather.5.cloned.1.call-update) | async-done | bytes 2359312 | tf_op jit(solution)/shard_map/all_gather | solution.py:132
  216.5 3.5 copy.111
  220.0 3.8 fusion.73
  223.8 2.4 copy.116
  226.2 3.0 fusion.72
  229.1 1.5 copy.113
  230.7 2.4 bitcast_multiply_fusion.3
  239.0 66.6 %all-reduce.10.cloned.1.call-done = (bf16[128,128]{1,0:T(8,128)(2,1)}, bf16[128,128]{1,0:T(8,128)(2,1)}, bf16[128]{0:T(256)(128)(2,1)}, bf16[128]{0:T(256)(128)(2,1)}) async-done(((bf16[128,128]{1,0:T(8,128)(2,1)}, bf16[128,128]{1,0:T(8,128)(2,1)}, bf16[128]{0:T(256)(128)(2,1)}, bf16[128]{0:T(256)(128)(2,1)}), (bf16[128,128]{1,0:T(8,128)(2,1)}, bf16[128,128]{1,0:T(8,128)(2,1)}, bf16[128]{0:T(256)(128)(2,1)}, ...) | async-done | bytes 66064 | tf_op jit(solution)/shard_map/psum | solution.py:145
  310.7 69.2 %all-reduce.8.cloned.1.call-done = bf16[128,512]{1,0:T(8,128)(2,1)} async-done(((bf16[128,512]{1,0:T(8,128)(2,1)}), bf16[128,512]{1,0:T(8,128)(2,1)}) %all-reduce.8.cloned.1.call-update) | async-done | bytes 131088 | tf_op jit(solution)/shard_map/psum | solution.py:144
  380.0 1.6 convert_element_type.107
  (168 shorter events, 58.2 us)
Async XLA Ops:
  7.2 73.9 %copy-start = (bf16[128,512]{1,0:T(8,128)(2,1)S(1)}, bf16[128,512]{1,0:T(8,128)(2,1)}, u32[]{:S(2)}) copy-start(bf16[128,512]{1,0:T(8,128)(2,1)} %param.26) | copy-start | bytes 393220
  7.2 64.5 %all-gather.3.cloned.1.call-start = ((), (), s32[]{:S(2)}) async-start(), calls=%async_computation.1 | async-start | bytes 2654208 | tf_op jit(solution)/shard_map/all_gather | solution.py:66
  13.9 67.6 %copy-start.25 = (f32[12,96]{1,0:T(8,128)}, f32[12,96]{1,0:T(8,128)S(1)}, u32[]{:S(2)}) copy-start(f32[12,96]{1,0:T(8,128)S(1)} %multiply_convert_fusion.10) | copy-start | bytes 13828
  15.9 2.3 copy-start.4
  75.2 3.1 copy-start.37
  78.1 2.6 copy-start.34
  80.3 2.9 copy-start.27
  81.1 12.4 %copy-start.13 = (bf16[12,96,128]{2,1,0:T(8,128)(2,1)}, bf16[12,96,128]{2,1,0:T(8,128)(2,1)S(1)}, u32[]{:S(2)}) copy-start(bf16[12,96,128]{2,1,0:T(8,128)(2,1)S(1)} %multiply_convert_fusion.4) | copy-start | bytes 884740
  82.9 10.5 %copy-start.30 = (bf16[128,128]{1,0:T(8,128)(2,1)S(1)}, bf16[128,128]{1,0:T(8,128)(2,1)}, u32[]{:S(2)}) copy-start(bf16[128,128]{1,0:T(8,128)(2,1)} %param.27) | copy-start | bytes 98308
  84.9 28.7 %all-to-all-start = ((bf16[12,96,128]{2,0,1:T(8,128)(2,1)}), bf16[12,96,128]{2,0,1:T(8,128)(2,1)S(1)}, u32[]{:S(2)}, u32[]{:S(2)}) async-start(bf16[12,96,128]{2,0,1:T(8,128)(2,1)} %copy.84), calls=%async_computation | async-start | bytes 786432 | tf_op jit(solution)/shard_map/all_to_all | solution.py:83
  88.3 128.2 %all-gather.5.cloned.1.call-start = ((), (), s32[]{:S(2)}) async-start(), calls=%async_computation.2 | async-start | bytes 2654208 | tf_op jit(solution)/shard_map/all_gather | solution.py:132
  88.4 19.6 %collective-permute-start = (bf16[12,96,128]{2,1,0:T(8,128)(2,1)S(1)}, bf16[12,96,128]{2,1,0:T(8,128)(2,1)}, u32[]{:S(2)}, u32[]{:S(2)}) collective-permute-start(bf16[12,96,128]{2,1,0:T(8,128)(2,1)S(1)} %get-tuple-element.25), channel_id=1, source_target_pairs={{0,28},{4,0},{8,4},{12,8},{16,12},{20,16},{24,20},{28,24},{1,29},{... | collective-permute-start | bytes 884744 | tf_op jit(solution)/shard_map/ppermute | solution.py:99
  93.0 17.4 %collective-permute-start.1 = (bf16[12,96,128]{2,1,0:T(8,128)(2,1)S(1)}, bf16[12,96,128]{2,1,0:T(8,128)(2,1)}, u32[]{:S(2)}, u32[]{:S(2)}) collective-permute-start(bf16[12,96,128]{2,1,0:T(8,128)(2,1)S(1)} %get-tuple-element.25), channel_id=1, source_target_pairs={{0,4},{4,8},{8,12},{12,16},{16,20},{20,24},{24,28},{28,0},{1,5},{5... | collective-permute-start | bytes 884744 | tf_op jit(solution)/shard_map/ppermute | solution.py:97
  93.4 27.9 %copy-start.8 = (bf16[12,96,128]{1,0,2:T(8,128)(2,1)}, bf16[12,96,128]{1,0,2:T(8,128)(2,1)S(1)}, u32[]{:S(2)}) copy-start(bf16[12,96,128]{1,0,2:T(8,128)(2,1)S(1)} %copy.88) | copy-start | bytes 884740
  109.4 18.9 %collective-permute-start.2 = (bf16[12,96,128]{2,1,0:T(8,128)(2,1)}, bf16[12,96,128]{2,1,0:T(8,128)(2,1)}, u32[]{:S(2)}, u32[]{:S(2)}) collective-permute-start(bf16[12,96,128]{2,1,0:T(8,128)(2,1)} %collective-permute-done), channel_id=1, source_target_pairs={{0,28},{4,0},{8,4},{12,8},{16,12},{20,16},{24,20},{28,24},{1,29},{... | collective-permute-start | bytes 884744 | tf_op jit(solution)/shard_map/ppermute | solution.py:99
  112.5 21.6 %collective-permute-start.3 = (bf16[12,96,128]{2,1,0:T(8,128)(2,1)}, bf16[12,96,128]{2,1,0:T(8,128)(2,1)}, u32[]{:S(2)}, u32[]{:S(2)}) collective-permute-start(bf16[12,96,128]{2,1,0:T(8,128)(2,1)} %collective-permute-done.1), channel_id=1, source_target_pairs={{0,4},{4,8},{8,12},{12,16},{16,20},{20,24},{24,28},{28,0},{1,5},{5... | collective-permute-start | bytes 884744 | tf_op jit(solution)/shard_map/ppermute | solution.py:97
  121.4 5.2 %copy-start.21 = (bf16[12,12,128]{2,0,1:T(8,128)(2,1)S(1)}, bf16[12,12,128]{2,0,1:T(8,128)(2,1)}, u32[]{:S(2)}) copy-start(bf16[12,12,128]{2,0,1:T(8,128)(2,1)} %get-tuple-element.29) | copy-start | bytes 110596
  121.7 4.4 %copy-start.22 = (bf16[12,12,128]{2,0,1:T(8,128)(2,1)S(1)}, bf16[12,12,128]{2,0,1:T(8,128)(2,1)}, u32[]{:S(2)}) copy-start(bf16[12,12,128]{2,0,1:T(8,128)(2,1)} %get-tuple-element.30) | copy-start | bytes 110596
  121.7 5.4 %copy-start.20 = (bf16[12,12,128]{2,0,1:T(8,128)(2,1)S(1)}, bf16[12,12,128]{2,0,1:T(8,128)(2,1)}, u32[]{:S(2)}) copy-start(bf16[12,12,128]{2,0,1:T(8,128)(2,1)} %get-tuple-element.35) | copy-start | bytes 110596
  130.5 11.1 %collective-permute-start.4 = (bf16[12,96,128]{2,1,0:T(8,128)(2,1)}, bf16[12,96,128]{2,1,0:T(8,128)(2,1)}, u32[]{:S(2)}, u32[]{:S(2)}) collective-permute-start(bf16[12,96,128]{2,1,0:T(8,128)(2,1)} %collective-permute-done.2), channel_id=1, source_target_pairs={{0,28},{4,0},{8,4},{12,8},{16,12},{20,16},{24,20},{28,24},{1,29},{... | collective-permute-start | bytes 884744 | tf_op jit(solution)/shard_map/ppermute | solution.py:99
  134.1 10.1 %collective-permute-start.5 = (bf16[12,96,128]{2,1,0:T(8,128)(2,1)}, bf16[12,96,128]{2,1,0:T(8,128)(2,1)}, u32[]{:S(2)}, u32[]{:S(2)}) collective-permute-start(bf16[12,96,128]{2,1,0:T(8,128)(2,1)} %collective-permute-done.3), channel_id=1, source_target_pairs={{0,4},{4,8},{8,12},{12,16},{16,20},{20,24},{24,28},{28,0},{1,5},{5... | collective-permute-start | bytes 884744 | tf_op jit(solution)/shard_map/ppermute | solution.py:97
  144.2 10.1 %collective-permute-start.6 = (bf16[12,96,128]{2,1,0:T(8,128)(2,1)}, bf16[12,96,128]{2,1,0:T(8,128)(2,1)}, u32[]{:S(2)}, u32[]{:S(2)}) collective-permute-start(bf16[12,96,128]{2,1,0:T(8,128)(2,1)} %collective-permute-done.5), channel_id=1, source_target_pairs={{0,4},{4,8},{8,12},{12,16},{16,20},{20,24},{24,28},{28,0},{1,5},{5... | collective-permute-start | bytes 884744 | tf_op jit(solution)/shard_map/ppermute | solution.py:97
  150.4 8.9 %copy-start.16 = (f32[128,96,12]{0,1,2:T(8,128)S(1)}, f32[128,96,12]{0,1,2:T(8,128)}, u32[]{:S(2)}) copy-start(f32[128,96,12]{0,1,2:T(8,128)} %copy.92) | copy-start | bytes 1769476
  150.4 8.9 %copy-start.17 = (f32[128,96,12]{0,1,2:T(8,128)S(1)}, f32[128,96,12]{0,1,2:T(8,128)}, u32[]{:S(2)}) copy-start(f32[128,96,12]{0,1,2:T(8,128)} %copy.95) | copy-start | bytes 1769476
  161.4 3.0 copy-start.10
  162.1 4.1 %copy-start.24 = (bf16[128,128]{1,0:T(8,128)(2,1)S(1)}, bf16[128,128]{1,0:T(8,128)(2,1)}, u32[]{:S(2)}) copy-start(bf16[128,128]{1,0:T(8,128)(2,1)} %param.29) | copy-start | bytes 98308
  162.2 4.1 %copy-start.33 = (f32[128]{0:T(128)S(1)}, f32[128]{0:T(128)}, u32[]{:S(2)}) copy-start(f32[128]{0:T(128)} %param.28) | copy-start | bytes 1540
  162.9 4.5 %copy-start.14 = (bf16[12,96,128]{2,1,0:T(8,128)(2,1)S(1)}, bf16[12,96,128]{2,1,0:T(8,128)(2,1)}, u32[]{:S(2)}) copy-start(bf16[12,96,128]{2,1,0:T(8,128)(2,1)} %copy-done.13) | copy-start | bytes 884740
  164.4 141.2 %all-reduce.10.cloned.1.call-start = ((), (), s32[]{:S(2)}) async-start(), calls=%async_computation.4 | async-start | bytes 133120 | tf_op jit(solution)/shard_map/psum | solution.py:145
  226.2 4.5 %copy-start.26 = (f32[12,96]{1,0:T(8,128)S(1)}, f32[12,96]{1,0:T(8,128)}, u32[]{:S(2)}) copy-start(f32[12,96]{1,0:T(8,128)} %copy-done.25) | copy-start | bytes 13828
  235.1 2.5 copy-start.7
  237.0 143.0 %all-reduce.8.cloned.1.call-start = ((), (), s32[]{:S(2)}) async-start(), calls=%async_computation.3 | async-start | bytes 262144 | tf_op jit(solution)/shard_map/psum | solution.py:144
  (19 other events, 26.2 us)
Sparse Core Ops, SparseCore 0:
  17.1 54.5 all-gather.2
  164.6 51.8 all-gather.4
  237.1 68.4 all-reduce.9
  309.4 70.4 all-reduce.7
